TPU v7x, 128 devices: a whole 4x4x4 slice. The times are simulated.
128 devices in a mesh: pz: 4 (over z), py: 4 (over y), px: 8 (over x, core).
Axes of the slice: x: 4, y: 4, z: 4, core: 2. Of those that a mesh axis runs over, the one named last changes fastest.
Arguments:
- shift_diag: float32 [2, 384, 192, 384], P(None, 'px', 'py', 'pz')
- rhs_field: float32 [2, 384, 192, 384], P(None, 'px', 'py', 'pz')
- x_start: float32 [2, 384, 192, 384], P(None, 'px', 'py', 'pz')
- cond_x: float32 [2, 384, 192, 384], P(None, 'px', 'py', 'pz')
- cond_y: float32 [2, 384, 192, 384], P(None, 'px', 'py', 'pz')
- cond_z: float32 [2, 384, 192, 384], P(None, 'px', 'py', 'pz')
Outputs:
- output 1: float32 [2, 384, 192, 384], P(None, 'px', 'py', 'pz')
- output 2: float32 [2, 21], replicated
All inputs are finite; a program needn't handle non-finite values.
Results may differ from a plain program's by a relative error of at most 0.001.
Values sent between devices are 32-bit elements.
A program may use at most 1 GiB of HBM per device.

v0:
```python
import jax
import jax.numpy as jnp
from jax import lax
from jax.sharding import PartitionSpec as P

ITERS = 20
GRID_AXES = ('px', 'py', 'pz')
ALL_AXES = ('pz', 'py', 'px')


def up_pairs(axis_size):
    return [(dev_idx, dev_idx + 1) for dev_idx in range(axis_size - 1)]


def down_pairs(axis_size):
    return [(dev_idx, dev_idx - 1) for dev_idx in range(1, axis_size)]


def neighbour_planes(field, axis_name, axis_dim, axis_size):
    planes = field.shape[axis_dim]
    first_plane = lax.slice_in_dim(field, 0, 1, axis=axis_dim)
    last_plane = lax.slice_in_dim(field, planes - 1, planes, axis=axis_dim)
    from_below = lax.ppermute(last_plane, axis_name, up_pairs(axis_size))
    from_above = lax.ppermute(first_plane, axis_name, down_pairs(axis_size))
    return from_below, from_above


def extend_conduct(conduct, axis_name, axis_dim, axis_size):
    planes = conduct.shape[axis_dim]
    plane_index = lax.broadcasted_iota(jnp.int32, tuple(planes if pos_dim == axis_dim else 1 for pos_dim in range(conduct.ndim)), axis_dim)
    at_edge = jnp.logical_and(lax.axis_index(axis_name) == axis_size - 1, plane_index == planes - 1)
    masked = jnp.where(at_edge, 0.0, conduct)
    lower_faces = lax.ppermute(lax.slice_in_dim(conduct, planes - 1, planes, axis=axis_dim), axis_name, up_pairs(axis_size))
    return jnp.concatenate([lower_faces, masked], axis=axis_dim)


def apply_local(field, shift_diag, cond_ext, axis_sizes):
    halo_pairs = [neighbour_planes(field, GRID_AXES[axis_pos], axis_pos + 1, axis_sizes[axis_pos]) for axis_pos in range(3)]
    result = shift_diag * field
    for axis_pos in range(3):
        axis_dim = axis_pos + 1
        planes = field.shape[axis_dim]
        padded = jnp.concatenate([halo_pairs[axis_pos][0], field, halo_pairs[axis_pos][1]], axis=axis_dim)
        face_flux = cond_ext[axis_pos] * (lax.slice_in_dim(padded, 0, planes + 1, axis=axis_dim) - lax.slice_in_dim(padded, 1, planes + 2, axis=axis_dim))
        result = result + (lax.slice_in_dim(face_flux, 1, planes + 1, axis=axis_dim) - lax.slice_in_dim(face_flux, 0, planes, axis=axis_dim))
    return result


def solution(mesh):
    axis_sizes = tuple(mesh.shape[axis_name] for axis_name in GRID_AXES)
    field_spec = P(None, 'px', 'py', 'pz')

    def local_solve(shift_diag, rhs_field, x_start, cond_x, cond_y, cond_z):
        cell_count = x_start.shape[1] * x_start.shape[2] * x_start.shape[3] * axis_sizes[0] * axis_sizes[1] * axis_sizes[2]
        cond_ext = [extend_conduct(conduct, GRID_AXES[axis_pos], axis_pos + 1, axis_sizes[axis_pos]) for axis_pos, conduct in enumerate((cond_x, cond_y, cond_z))]

        def global_dot(left_vec, right_vec):
            return lax.psum(jnp.sum(left_vec * right_vec, axis=(1, 2, 3)), ALL_AXES)

        residual = rhs_field - apply_local(x_start, shift_diag, cond_ext, axis_sizes)
        rho_start = global_dot(residual, residual)

        def cg_step(loop_state, unused):
            x_cur, res_cur, direction, rho_old, beta_coef = loop_state
            direction = res_cur + beta_coef[:, None, None, None] * direction
            q_vec = apply_local(direction, shift_diag, cond_ext, axis_sizes)
            alpha_step = rho_old / global_dot(direction, q_vec)
            x_cur = x_cur + alpha_step[:, None, None, None] * direction
            res_cur = res_cur - alpha_step[:, None, None, None] * q_vec
            rho_new = global_dot(res_cur, res_cur)
            return (x_cur, res_cur, direction, rho_new, rho_new / rho_old), jnp.sqrt(rho_new / cell_count)

        init_state = (x_start, residual, jnp.zeros_like(residual), rho_start, jnp.zeros_like(rho_start))
        final_state, res_tail = lax.scan(cg_step, init_state, None, length=ITERS)
        res_hist = jnp.concatenate([jnp.sqrt(rho_start / cell_count)[None], res_tail], axis=0).T
        return final_state[0], res_hist

    return jax.shard_map(local_solve, mesh=mesh, in_specs=(field_spec, field_spec, field_spec, field_spec, field_spec, field_spec), out_specs=(field_spec, P(None, None)), check_vma=False)
```

profile of v0, /device:TPU:1, one launch (start us, length us, event | category | flops | bytes accessed | tf_op | source)
XLA Modules:
  0.0 3620.0 jit_solution(13530652169784052787)
XLA Ops:
  62.3 7.0 fusion.13
  85.7 64.1 %psum.21 = f32[2]{0:T(128)S(1)} all-reduce(f32[2]{0:T(128)S(1)} %get-tuple-element.163), channel_id=1, replica_groups=mesh['pz'=4,'py'=4,'px'=8] {'pz','py','px'}, use_global_device_ids=true, to_apply=%region_1.2 | all-reduce | flops 2 | bytes 16 | tf_op jit(solution)/shard_map/psum | solution.py:58
  158.4 3457.0 %while.21 = (s32[]{:T(128)}, f32[2,48,48,96]{3,1,2,0:T(8,128)}, f32[2,48,48,96]{3,1,2,0:T(8,128)}, f32[2,48,48,96]{3,1,2,0:T(8,128)S(1)}, f32[2]{0:T(128)S(1)}, ...) while((s32[]{:T(128)}, f32[2,48,48,96]{3,1,2,0:T(8,128)}, ...), condition=%wide.region_7.8_spmd.clone, body=%wide.region_2.7_spmd.clone.sunk | while | flops 13363211 | bytes 70926976 | solution.py:74
  196.3 66.5 %psum.26 = f32[2]{0:T(128)S(1)} all-reduce(f32[2]{0:T(128)S(1)} %get-tuple-element.273), channel_id=1, replica_groups=mesh['pz'=4,'py'=4,'px'=8] {'pz','py','px'}, use_global_device_ids=true, to_apply=%region_4.4 | all-reduce | flops 2 | bytes 16 | tf_op jit(solution)/shard_map/while/body/eval_jaxpr/psum | solution.py:58
  262.9 5.7 multiply_reduce_fusion.6
  268.6 63.5 %psum.27 = f32[2]{0:T(128)S(1)} all-reduce(f32[2]{0:T(128)S(1)} %get-tuple-element.276), channel_id=1, replica_groups=mesh['pz'=4,'py'=4,'px'=8] {'pz','py','px'}, use_global_device_ids=true, to_apply=%region_6.6 | all-reduce | flops 2 | bytes 16 | tf_op jit(solution)/shard_map/while/body/eval_jaxpr/psum | solution.py:58
  368.9 66.4 %psum.26 = f32[2]{0:T(128)S(1)} all-reduce(f32[2]{0:T(128)S(1)} %get-tuple-element.273), channel_id=1, replica_groups=mesh['pz'=4,'py'=4,'px'=8] {'pz','py','px'}, use_global_device_ids=true, to_apply=%region_4.4 | all-reduce | flops 2 | bytes 16 | tf_op jit(solution)/shard_map/while/body/eval_jaxpr/psum | solution.py:58
  441.0 64.1 %psum.27 = f32[2]{0:T(128)S(1)} all-reduce(f32[2]{0:T(128)S(1)} %get-tuple-element.276), channel_id=1, replica_groups=mesh['pz'=4,'py'=4,'px'=8] {'pz','py','px'}, use_global_device_ids=true, to_apply=%region_6.6 | all-reduce | flops 2 | bytes 16 | tf_op jit(solution)/shard_map/while/body/eval_jaxpr/psum | solution.py:58
  541.5 67.3 %psum.26 = f32[2]{0:T(128)S(1)} all-reduce(f32[2]{0:T(128)S(1)} %get-tuple-element.273), channel_id=1, replica_groups=mesh['pz'=4,'py'=4,'px'=8] {'pz','py','px'}, use_global_device_ids=true, to_apply=%region_4.4 | all-reduce | flops 2 | bytes 16 | tf_op jit(solution)/shard_map/while/body/eval_jaxpr/psum | solution.py:58
  608.8 5.7 multiply_reduce_fusion.6
  614.5 63.4 %psum.27 = f32[2]{0:T(128)S(1)} all-reduce(f32[2]{0:T(128)S(1)} %get-tuple-element.276), channel_id=1, replica_groups=mesh['pz'=4,'py'=4,'px'=8] {'pz','py','px'}, use_global_device_ids=true, to_apply=%region_6.6 | all-reduce | flops 2 | bytes 16 | tf_op jit(solution)/shard_map/while/body/eval_jaxpr/psum | solution.py:58
  714.4 67.5 %psum.26 = f32[2]{0:T(128)S(1)} all-reduce(f32[2]{0:T(128)S(1)} %get-tuple-element.273), channel_id=1, replica_groups=mesh['pz'=4,'py'=4,'px'=8] {'pz','py','px'}, use_global_device_ids=true, to_apply=%region_4.4 | all-reduce | flops 2 | bytes 16 | tf_op jit(solution)/shard_map/while/body/eval_jaxpr/psum | solution.py:58
  787.6 63.1 %psum.27 = f32[2]{0:T(128)S(1)} all-reduce(f32[2]{0:T(128)S(1)} %get-tuple-element.276), channel_id=1, replica_groups=mesh['pz'=4,'py'=4,'px'=8] {'pz','py','px'}, use_global_device_ids=true, to_apply=%region_6.6 | all-reduce | flops 2 | bytes 16 | tf_op jit(solution)/shard_map/while/body/eval_jaxpr/psum | solution.py:58
  887.6 66.5 %psum.26 = f32[2]{0:T(128)S(1)} all-reduce(f32[2]{0:T(128)S(1)} %get-tuple-element.273), channel_id=1, replica_groups=mesh['pz'=4,'py'=4,'px'=8] {'pz','py','px'}, use_global_device_ids=true, to_apply=%region_4.4 | all-reduce | flops 2 | bytes 16 | tf_op jit(solution)/shard_map/while/body/eval_jaxpr/psum | solution.py:58
  954.1 5.7 multiply_reduce_fusion.6
  959.8 63.7 %psum.27 = f32[2]{0:T(128)S(1)} all-reduce(f32[2]{0:T(128)S(1)} %get-tuple-element.276), channel_id=1, replica_groups=mesh['pz'=4,'py'=4,'px'=8] {'pz','py','px'}, use_global_device_ids=true, to_apply=%region_6.6 | all-reduce | flops 2 | bytes 16 | tf_op jit(solution)/shard_map/while/body/eval_jaxpr/psum | solution.py:58
  1060.1 67.4 %psum.26 = f32[2]{0:T(128)S(1)} all-reduce(f32[2]{0:T(128)S(1)} %get-tuple-element.273), channel_id=1, replica_groups=mesh['pz'=4,'py'=4,'px'=8] {'pz','py','px'}, use_global_device_ids=true, to_apply=%region_4.4 | all-reduce | flops 2 | bytes 16 | tf_op jit(solution)/shard_map/while/body/eval_jaxpr/psum | solution.py:58
  1133.2 63.1 %psum.27 = f32[2]{0:T(128)S(1)} all-reduce(f32[2]{0:T(128)S(1)} %get-tuple-element.276), channel_id=1, replica_groups=mesh['pz'=4,'py'=4,'px'=8] {'pz','py','px'}, use_global_device_ids=true, to_apply=%region_6.6 | all-reduce | flops 2 | bytes 16 | tf_op jit(solution)/shard_map/while/body/eval_jaxpr/psum | solution.py:58
  1233.2 66.6 %psum.26 = f32[2]{0:T(128)S(1)} all-reduce(f32[2]{0:T(128)S(1)} %get-tuple-element.273), channel_id=1, replica_groups=mesh['pz'=4,'py'=4,'px'=8] {'pz','py','px'}, use_global_device_ids=true, to_apply=%region_4.4 | all-reduce | flops 2 | bytes 16 | tf_op jit(solution)/shard_map/while/body/eval_jaxpr/psum | solution.py:58
  1299.7 5.7 multiply_reduce_fusion.6
  1305.4 63.7 %psum.27 = f32[2]{0:T(128)S(1)} all-reduce(f32[2]{0:T(128)S(1)} %get-tuple-element.276), channel_id=1, replica_groups=mesh['pz'=4,'py'=4,'px'=8] {'pz','py','px'}, use_global_device_ids=true, to_apply=%region_6.6 | all-reduce | flops 2 | bytes 16 | tf_op jit(solution)/shard_map/while/body/eval_jaxpr/psum | solution.py:58
  1405.7 67.4 %psum.26 = f32[2]{0:T(128)S(1)} all-reduce(f32[2]{0:T(128)S(1)} %get-tuple-element.273), channel_id=1, replica_groups=mesh['pz'=4,'py'=4,'px'=8] {'pz','py','px'}, use_global_device_ids=true, to_apply=%region_4.4 | all-reduce | flops 2 | bytes 16 | tf_op jit(solution)/shard_map/while/body/eval_jaxpr/psum | solution.py:58
  1473.1 5.7 multiply_reduce_fusion.6
  1478.8 63.1 %psum.27 = f32[2]{0:T(128)S(1)} all-reduce(f32[2]{0:T(128)S(1)} %get-tuple-element.276), channel_id=1, replica_groups=mesh['pz'=4,'py'=4,'px'=8] {'pz','py','px'}, use_global_device_ids=true, to_apply=%region_6.6 | all-reduce | flops 2 | bytes 16 | tf_op jit(solution)/shard_map/while/body/eval_jaxpr/psum | solution.py:58
  1578.7 66.6 %psum.26 = f32[2]{0:T(128)S(1)} all-reduce(f32[2]{0:T(128)S(1)} %get-tuple-element.273), channel_id=1, replica_groups=mesh['pz'=4,'py'=4,'px'=8] {'pz','py','px'}, use_global_device_ids=true, to_apply=%region_4.4 | all-reduce | flops 2 | bytes 16 | tf_op jit(solution)/shard_map/while/body/eval_jaxpr/psum | solution.py:58
  1651.0 63.7 %psum.27 = f32[2]{0:T(128)S(1)} all-reduce(f32[2]{0:T(128)S(1)} %get-tuple-element.276), channel_id=1, replica_groups=mesh['pz'=4,'py'=4,'px'=8] {'pz','py','px'}, use_global_device_ids=true, to_apply=%region_6.6 | all-reduce | flops 2 | bytes 16 | tf_op jit(solution)/shard_map/while/body/eval_jaxpr/psum | solution.py:58
  1751.2 67.4 %psum.26 = f32[2]{0:T(128)S(1)} all-reduce(f32[2]{0:T(128)S(1)} %get-tuple-element.273), channel_id=1, replica_groups=mesh['pz'=4,'py'=4,'px'=8] {'pz','py','px'}, use_global_device_ids=true, to_apply=%region_4.4 | all-reduce | flops 2 | bytes 16 | tf_op jit(solution)/shard_map/while/body/eval_jaxpr/psum | solution.py:58
  1824.4 63.1 %psum.27 = f32[2]{0:T(128)S(1)} all-reduce(f32[2]{0:T(128)S(1)} %get-tuple-element.276), channel_id=1, replica_groups=mesh['pz'=4,'py'=4,'px'=8] {'pz','py','px'}, use_global_device_ids=true, to_apply=%region_6.6 | all-reduce | flops 2 | bytes 16 | tf_op jit(solution)/shard_map/while/body/eval_jaxpr/psum | solution.py:58
  1924.3 66.6 %psum.26 = f32[2]{0:T(128)S(1)} all-reduce(f32[2]{0:T(128)S(1)} %get-tuple-element.273), channel_id=1, replica_groups=mesh['pz'=4,'py'=4,'px'=8] {'pz','py','px'}, use_global_device_ids=true, to_apply=%region_4.4 | all-reduce | flops 2 | bytes 16 | tf_op jit(solution)/shard_map/while/body/eval_jaxpr/psum | solution.py:58
  1996.6 63.7 %psum.27 = f32[2]{0:T(128)S(1)} all-reduce(f32[2]{0:T(128)S(1)} %get-tuple-element.276), channel_id=1, replica_groups=mesh['pz'=4,'py'=4,'px'=8] {'pz','py','px'}, use_global_device_ids=true, to_apply=%region_6.6 | all-reduce | flops 2 | bytes 16 | tf_op jit(solution)/shard_map/while/body/eval_jaxpr/psum | solution.py:58
  2096.8 67.4 %psum.26 = f32[2]{0:T(128)S(1)} all-reduce(f32[2]{0:T(128)S(1)} %get-tuple-element.273), channel_id=1, replica_groups=mesh['pz'=4,'py'=4,'px'=8] {'pz','py','px'}, use_global_device_ids=true, to_apply=%region_4.4 | all-reduce | flops 2 | bytes 16 | tf_op jit(solution)/shard_map/while/body/eval_jaxpr/psum | solution.py:58
  2169.9 63.1 %psum.27 = f32[2]{0:T(128)S(1)} all-reduce(f32[2]{0:T(128)S(1)} %get-tuple-element.276), channel_id=1, replica_groups=mesh['pz'=4,'py'=4,'px'=8] {'pz','py','px'}, use_global_device_ids=true, to_apply=%region_6.6 | all-reduce | flops 2 | bytes 16 | tf_op jit(solution)/shard_map/while/body/eval_jaxpr/psum | solution.py:58
  2269.9 66.6 %psum.26 = f32[2]{0:T(128)S(1)} all-reduce(f32[2]{0:T(128)S(1)} %get-tuple-element.273), channel_id=1, replica_groups=mesh['pz'=4,'py'=4,'px'=8] {'pz','py','px'}, use_global_device_ids=true, to_apply=%region_4.4 | all-reduce | flops 2 | bytes 16 | tf_op jit(solution)/shard_map/while/body/eval_jaxpr/psum | solution.py:58
  2342.2 63.7 %psum.27 = f32[2]{0:T(128)S(1)} all-reduce(f32[2]{0:T(128)S(1)} %get-tuple-element.276), channel_id=1, replica_groups=mesh['pz'=4,'py'=4,'px'=8] {'pz','py','px'}, use_global_device_ids=true, to_apply=%region_6.6 | all-reduce | flops 2 | bytes 16 | tf_op jit(solution)/shard_map/while/body/eval_jaxpr/psum | solution.py:58
  2442.4 67.4 %psum.26 = f32[2]{0:T(128)S(1)} all-reduce(f32[2]{0:T(128)S(1)} %get-tuple-element.273), channel_id=1, replica_groups=mesh['pz'=4,'py'=4,'px'=8] {'pz','py','px'}, use_global_device_ids=true, to_apply=%region_4.4 | all-reduce | flops 2 | bytes 16 | tf_op jit(solution)/shard_map/while/body/eval_jaxpr/psum | solution.py:58
  2515.5 63.1 %psum.27 = f32[2]{0:T(128)S(1)} all-reduce(f32[2]{0:T(128)S(1)} %get-tuple-element.276), channel_id=1, replica_groups=mesh['pz'=4,'py'=4,'px'=8] {'pz','py','px'}, use_global_device_ids=true, to_apply=%region_6.6 | all-reduce | flops 2 | bytes 16 | tf_op jit(solution)/shard_map/while/body/eval_jaxpr/psum | solution.py:58
  2615.5 66.6 %psum.26 = f32[2]{0:T(128)S(1)} all-reduce(f32[2]{0:T(128)S(1)} %get-tuple-element.273), channel_id=1, replica_groups=mesh['pz'=4,'py'=4,'px'=8] {'pz','py','px'}, use_global_device_ids=true, to_apply=%region_4.4 | all-reduce | flops 2 | bytes 16 | tf_op jit(solution)/shard_map/while/body/eval_jaxpr/psum | solution.py:58
  2687.8 63.7 %psum.27 = f32[2]{0:T(128)S(1)} all-reduce(f32[2]{0:T(128)S(1)} %get-tuple-element.276), channel_id=1, replica_groups=mesh['pz'=4,'py'=4,'px'=8] {'pz','py','px'}, use_global_device_ids=true, to_apply=%region_6.6 | all-reduce | flops 2 | bytes 16 | tf_op jit(solution)/shard_map/while/body/eval_jaxpr/psum | solution.py:58
  2788.0 67.4 %psum.26 = f32[2]{0:T(128)S(1)} all-reduce(f32[2]{0:T(128)S(1)} %get-tuple-element.273), channel_id=1, replica_groups=mesh['pz'=4,'py'=4,'px'=8] {'pz','py','px'}, use_global_device_ids=true, to_apply=%region_4.4 | all-reduce | flops 2 | bytes 16 | tf_op jit(solution)/shard_map/while/body/eval_jaxpr/psum | solution.py:58
  2861.1 63.1 %psum.27 = f32[2]{0:T(128)S(1)} all-reduce(f32[2]{0:T(128)S(1)} %get-tuple-element.276), channel_id=1, replica_groups=mesh['pz'=4,'py'=4,'px'=8] {'pz','py','px'}, use_global_device_ids=true, to_apply=%region_6.6 | all-reduce | flops 2 | bytes 16 | tf_op jit(solution)/shard_map/while/body/eval_jaxpr/psum | solution.py:58
  2961.1 66.6 %psum.26 = f32[2]{0:T(128)S(1)} all-reduce(f32[2]{0:T(128)S(1)} %get-tuple-element.273), channel_id=1, replica_groups=mesh['pz'=4,'py'=4,'px'=8] {'pz','py','px'}, use_global_device_ids=true, to_apply=%region_4.4 | all-reduce | flops 2 | bytes 16 | tf_op jit(solution)/shard_map/while/body/eval_jaxpr/psum | solution.py:58
  3033.4 63.7 %psum.27 = f32[2]{0:T(128)S(1)} all-reduce(f32[2]{0:T(128)S(1)} %get-tuple-element.276), channel_id=1, replica_groups=mesh['pz'=4,'py'=4,'px'=8] {'pz','py','px'}, use_global_device_ids=true, to_apply=%region_6.6 | all-reduce | flops 2 | bytes 16 | tf_op jit(solution)/shard_map/while/body/eval_jaxpr/psum | solution.py:58
  3133.6 67.4 %psum.26 = f32[2]{0:T(128)S(1)} all-reduce(f32[2]{0:T(128)S(1)} %get-tuple-element.273), channel_id=1, replica_groups=mesh['pz'=4,'py'=4,'px'=8] {'pz','py','px'}, use_global_device_ids=true, to_apply=%region_4.4 | all-reduce | flops 2 | bytes 16 | tf_op jit(solution)/shard_map/while/body/eval_jaxpr/psum | solution.py:58
  3206.7 63.1 %psum.27 = f32[2]{0:T(128)S(1)} all-reduce(f32[2]{0:T(128)S(1)} %get-tuple-element.276), channel_id=1, replica_groups=mesh['pz'=4,'py'=4,'px'=8] {'pz','py','px'}, use_global_device_ids=true, to_apply=%region_6.6 | all-reduce | flops 2 | bytes 16 | tf_op jit(solution)/shard_map/while/body/eval_jaxpr/psum | solution.py:58
  3306.7 66.6 %psum.26 = f32[2]{0:T(128)S(1)} all-reduce(f32[2]{0:T(128)S(1)} %get-tuple-element.273), channel_id=1, replica_groups=mesh['pz'=4,'py'=4,'px'=8] {'pz','py','px'}, use_global_device_ids=true, to_apply=%region_4.4 | all-reduce | flops 2 | bytes 16 | tf_op jit(solution)/shard_map/while/body/eval_jaxpr/psum | solution.py:58
  3378.9 63.7 %psum.27 = f32[2]{0:T(128)S(1)} all-reduce(f32[2]{0:T(128)S(1)} %get-tuple-element.276), channel_id=1, replica_groups=mesh['pz'=4,'py'=4,'px'=8] {'pz','py','px'}, use_global_device_ids=true, to_apply=%region_6.6 | all-reduce | flops 2 | bytes 16 | tf_op jit(solution)/shard_map/while/body/eval_jaxpr/psum | solution.py:58
  3479.2 67.4 %psum.26 = f32[2]{0:T(128)S(1)} all-reduce(f32[2]{0:T(128)S(1)} %get-tuple-element.273), channel_id=1, replica_groups=mesh['pz'=4,'py'=4,'px'=8] {'pz','py','px'}, use_global_device_ids=true, to_apply=%region_4.4 | all-reduce | flops 2 | bytes 16 | tf_op jit(solution)/shard_map/while/body/eval_jaxpr/psum | solution.py:58
  3552.3 63.1 %psum.27 = f32[2]{0:T(128)S(1)} all-reduce(f32[2]{0:T(128)S(1)} %get-tuple-element.276), channel_id=1, replica_groups=mesh['pz'=4,'py'=4,'px'=8] {'pz','py','px'}, use_global_device_ids=true, to_apply=%region_6.6 | all-reduce | flops 2 | bytes 16 | tf_op jit(solution)/shard_map/while/body/eval_jaxpr/psum | solution.py:58
  (788 shorter events, 907.9 us)
Async XLA Ops:
  4.6 69.0 %collective-permute-start.10 = (f32[2,48,1,96]{3,1,2,0:T(8,128)S(1)}, f32[2,48,1,96]{3,1,2,0:T(8,128)S(1)}, u32[]{:S(2)}, u32[]{:S(2)}) collective-permute-start(f32[2,48,1,96]{3,1,2,0:T(8,128)S(1)} %get-tuple-element.183), channel_id=1, source_target_pairs={{0,8},{8,16},{16,24},{1,9},{9,17},{17,25},{2,10},{10,18},{18,26},{... | collective-permute-start | bytes 110600 | tf_op jit(solution)/shard_map/ppermute | solution.py:23
  14.0 32.4 collective-permute-start.13
  20.1 32.6 collective-permute-start.14
  27.6 32.5 collective-permute-start.12
  45.1 32.1 collective-permute-start.11
  48.6 28.6 collective-permute-start.9
  54.9 24.9 collective-permute-start.7
  166.0 13.8 collective-permute-start
  172.7 17.6 collective-permute-start.4
  176.0 14.3 collective-permute-start.5
  345.7 17.2 collective-permute-start.4
  348.5 14.3 collective-permute-start.5
  518.4 17.1 collective-permute-start.4
  521.6 13.9 collective-permute-start.5
  691.3 17.1 collective-permute-start.4
  694.5 13.9 collective-permute-start.5
  864.3 17.2 collective-permute-start.4
  867.2 14.3 collective-permute-start.5
  1037.1 16.9 collective-permute-start.4
  1040.1 13.9 collective-permute-start.5
  1209.9 17.2 collective-permute-start.4
  1212.8 14.3 collective-permute-start.5
  1382.6 17.0 collective-permute-start.4
  1385.7 13.9 collective-permute-start.5
  1555.5 17.2 collective-permute-start.4
  1558.4 14.3 collective-permute-start.5
  1728.2 16.9 collective-permute-start.4
  1731.3 13.9 collective-permute-start.5
  1901.0 17.2 collective-permute-start.4
  1904.0 14.3 collective-permute-start.5
  2073.8 17.0 collective-permute-start.4
  2076.9 13.9 collective-permute-start.5
  2246.6 17.2 collective-permute-start.4
  2249.6 14.3 collective-permute-start.5
  2419.4 16.9 collective-permute-start.4
  2422.5 13.9 collective-permute-start.5
  2592.2 17.2 collective-permute-start.4
  2595.1 14.3 collective-permute-start.5
  2765.0 16.9 collective-permute-start.4
  2768.0 13.9 collective-permute-start.5
  2937.8 17.2 collective-permute-start.4
  2940.7 14.3 collective-permute-start.5
  3110.6 16.9 collective-permute-start.4
  3113.6 13.9 collective-permute-start.5
  3283.4 17.2 collective-permute-start.4
  3286.3 14.3 collective-permute-start.5
  3456.1 16.9 collective-permute-start.4
  3459.2 13.9 collective-permute-start.5
  (151 other events, 1165.2 us)
where the time goes:
time: 3630 us; the launch traced here: 3620 us
  blocking collectives  2670 us (74%)
  local copies, waits for them, and re-layouts  348 us (10%)
  other arithmetic  343 us (9%)
  starting transfers between devices  251 us (7%)
    psum x41, blocking collectives, global_dot(): return lax.psum(jnp.sum(left_vec * right_vec, axis=(1, 2, 3)), ALL_AXES)  2670 us
    reduce_sum x41, other arithmetic, global_dot(): return lax.psum(jnp.sum(left_vec * right_vec, axis=(1, 2, 3)), ALL_AXES)  170 us
    ppermute x63, starting transfers between devices, neighbour_planes(): from_below = lax.ppermute(last_plane, axis_name, up_pairs(axis_size))  145 us
    mul x61, other arithmetic, apply_local(): cond_ext[axis_pos]  117 us
    slice x83, local copies, waits for them, and re-layouts, neighbour_planes(): first_plane = lax.slice_in_dim(field, 0, 1, axis=axis_dim)  115 us
    ppermute x63, starting transfers between devices, neighbour_planes(): from_above = lax.ppermute(first_plane, axis_name, down_pairs(axis_size))  94.5 us
  transfers between devices with their start and end apart: 129, of which 0 were waited for; matrix products, arithmetic and copies ran while one was open for 8% of the time, Pallas kernels for 0%

commit v1 on v0

v1 whole, which is shorter than its diff:
```python
import functools
import itertools

import jax
import jax.numpy as jnp
from jax import lax
from jax.experimental import pallas as pl
from jax.experimental.pallas import tpu as pltpu
from jax.sharding import PartitionSpec as P

ITERS = 20
SYS = 2
ROW0 = 8
LANES = 128
MESH = pl.DeviceIdType.MESH
PQ, RR, RR0 = 0, 1, 2


def far_first(nx, ny, nz):
    def route(offset):
        hops = sum(min(step, size - step) for step, size in zip(offset[1:], (nx // 2, ny, nz)))
        return (hops, offset[0])
    offsets = [offset for offset in itertools.product(range(2), range(nx // 2), range(ny), range(nz)) if any(offset)]
    return sorted(offsets, key=route, reverse=True)


def cg_kernel(axis_sizes, block, cell_count,
              s_ref, b_ref, x0_ref, kx_ref, ky_ref, kz_ref,
              x_ref, hist_out,
              r, p, q, kyd, kze, kx0,
              dot_send, dot_recv, rho_ref, beta_ref, hist_ref,
              y_send, y_recv, z_send, z_recv,
              yi_send, yi_recv, zi_send, zi_recv,
              dot_ssem, dot_rsem, halo_ssem, halo_rsem, init_ssem, init_rsem):
    nx, ny, nz = axis_sizes
    bx, by, bz = block
    n_dev = nx * ny * nz
    px, py, pz = lax.axis_index('px'), lax.axis_index('py'), lax.axis_index('pz')
    me = (pz * ny + py) * nx + px
    rows = pl.ds(ROW0, by)
    half = bx // 2
    lane_plane = lax.broadcasted_iota(jnp.int32, (by, LANES), 1)
    lane_row = lax.broadcasted_iota(jnp.int32, (1, LANES), 1)

    def device(x_pos, y_pos, z_pos):
        return {'px': x_pos, 'py': y_pos, 'pz': z_pos}

    x_up, x_dn = device(lax.rem(px + 1, nx), py, pz), device(lax.rem(px + nx - 1, nx), py, pz)
    y_up, y_dn = device(px, lax.rem(py + 1, ny), pz), device(px, lax.rem(py + ny - 1, ny), pz)
    z_up, z_dn = device(px, py, lax.rem(pz + 1, nz)), device(px, py, lax.rem(pz + nz - 1, nz))

    core, chip = lax.rem(px, 2), lax.div(px, 2)
    part_z = [lax.rem(pz + step, nz) for step in range(nz)]
    part_y = [lax.rem(py + step, ny) for step in range(ny)]
    part_x = [[lax.rem(chip + step, nx // 2) * 2 + lax.rem(core + flip, 2) for step in range(nx // 2)] for flip in range(2)]
    targets = far_first(nx, ny, nz)

    def remote(src, dst, send_sem, recv_sem, dev):
        return pltpu.make_async_remote_copy(src_ref=src, dst_ref=dst, send_sem=send_sem, recv_sem=recv_sem, device_id=dev, device_id_type=MESH)

    def dot_start(c, slot, acc):
        total = jnp.sum(jnp.sum(acc, axis=0, keepdims=True), axis=1, keepdims=True)
        row = jnp.broadcast_to(total, (1, LANES))
        dot_send[c, slot] = row
        dot_recv[c, slot, me] = row
        for flip, step_x, step_y, step_z in targets:
            dev = device(part_x[flip][step_x], part_y[step_y], part_z[step_z])
            remote(dot_send.at[c, slot], dot_recv.at[c, slot, me], dot_ssem.at[c, slot], dot_rsem.at[c, slot], dev).start()

    def dot_wait(c, slot):
        others = dot_recv.at[c, slot, pl.ds(0, n_dev - 1)]
        pltpu.make_async_copy(others, others, dot_rsem.at[c, slot]).wait()
        pltpu.make_async_copy(others, others, dot_ssem.at[c, slot]).wait()
        return jnp.sum(dot_recv[c, slot], axis=0)

    def z_shift(a):
        return a + 33 + jnp.where(a >= half, 64 - half, 0)

    def z_extract(load):
        def body(a, packed):
            shift = z_shift(a)
            moved = pltpu.roll(load(a), shift, 1)
            pick = jnp.logical_or(lane_plane == shift, lane_plane == shift - 33)
            return jnp.where(pick, moved, packed)
        return lax.fori_loop(0, bx, body, jnp.zeros((by, LANES), jnp.float32), unroll=4)

    def z_insert(own, from_dn, from_up, store):
        from_dn = jnp.where(pz == 0, pltpu.roll(own, LANES - 33, 1), from_dn)
        from_up = jnp.where(pz == nz - 1, pltpu.roll(own, 33, 1), from_up)
        low_lanes = jnp.logical_or(jnp.logical_and(lane_plane >= 33, lane_plane < 33 + half),
                                   jnp.logical_and(lane_plane >= 97, lane_plane < 97 + half))
        both = jnp.where(low_lanes, from_up, pltpu.roll(from_dn, 64, 1))

        def body(a, carry):
            moved = pltpu.roll(both, lax.rem(96 + LANES - z_shift(a), LANES), 1)
            store(a, moved[:, bz:])
            return carry
        lax.fori_loop(0, bx, body, 0, unroll=4)

    def halo_copies(c, field, ys, yr, zs, zr, ssem, rsem):
        return [
            remote(field.at[c, 1, rows], field.at[c, bx + 1, rows], ssem.at[c, 0], rsem.at[c, 0], x_dn),
            remote(field.at[c, bx, rows], field.at[c, 0, rows], ssem.at[c, 1], rsem.at[c, 1], x_up),
            remote(ys.at[c, 0], yr.at[c, 0], ssem.at[c, 2], rsem.at[c, 2], y_dn),
            remote(ys.at[c, 1], yr.at[c, 1], ssem.at[c, 3], rsem.at[c, 3], y_up),
            remote(zs.at[c], zr.at[c, 0], ssem.at[c, 4], rsem.at[c, 4], z_dn),
            remote(zs.at[c], zr.at[c, 1], ssem.at[c, 5], rsem.at[c, 5], z_up),
        ]

    def halo_start(c, field, ys, yr, zs, zr, ssem, rsem):
        copies = halo_copies(c, field, ys, yr, zs, zr, ssem, rsem)
        copies[0].start()
        copies[1].start()

        def pack(a, carry):
            ys[c, 0, a] = field[c, a + 1, ROW0:ROW0 + 1, :]
            ys[c, 1, a] = field[c, a + 1, ROW0 + by - 1:ROW0 + by, :]
            return carry
        lax.fori_loop(0, bx, pack, 0, unroll=8)
        copies[2].start()
        copies[3].start()
        zs[c] = z_extract(lambda a: field[c, a + 1, ROW0:ROW0 + by, :])
        copies[4].start()
        copies[5].start()

    def halo_finish(c, field, ys, yr, zs, zr, ssem, rsem):
        for copy in halo_copies(c, field, ys, yr, zs, zr, ssem, rsem):
            copy.wait()

        @pl.when(px == nx - 1)
        def _():
            field[c, bx + 1, ROW0:ROW0 + by, :] = field[c, bx, ROW0:ROW0 + by, :]

        @pl.when(px == 0)
        def _():
            field[c, 0, ROW0:ROW0 + by, :] = field[c, 1, ROW0:ROW0 + by, :]

        def unpack(a, carry):
            field[c, a + 1, ROW0 + by:ROW0 + by + 1, :] = jnp.where(py == ny - 1, ys[c, 1, a], yr[c, 0, a])
            field[c, a + 1, ROW0 - 1:ROW0, :] = jnp.where(py == 0, ys[c, 0, a], yr[c, 1, a])
            return carry
        lax.fori_loop(0, bx, unpack, 0, unroll=8)

        def store(a, lanes):
            field[c, a + 1, ROW0:ROW0 + by, bz:] = lanes
        z_insert(zs[c], zr[c, 1], zr[c, 0], store)

    r_halo = (r, y_send, y_recv, z_send, z_recv, halo_ssem, halo_rsem)
    x_halo = (p, yi_send.at[0], yi_recv.at[0], zi_send.at[0], zi_recv.at[0], init_ssem.at[0], init_rsem.at[0])

    def apply(c, beta, with_dot):
        def direction(j):
            if beta is None:
                return p[c, j, ROW0:ROW0 + by, :]
            new = r[c, j] + beta * p[c, j]
            p[c, j] = new
            return new[ROW0:ROW0 + by, :]

        def flux_x(conduct, low, high):
            return conduct * (low[:, :bz] - high[:, :bz])

        below, first = direction(0), direction(1)

        def body(a, carry):
            here, flux_low, acc = carry
            above = direction(a + 2)
            mid = here[:, :bz]
            flux_high = flux_x(kx_ref[c, a], here, above)
            flux_y = ky_ref[c, a] * (mid - p[c, a + 1, ROW0 + 1:ROW0 + by + 1, :bz])
            flux_yd = kyd[c, a] * (p[c, a + 1, ROW0 - 1:ROW0 + by - 1, :bz] - mid)
            flux_z = kze[c, a] * (here - pltpu.roll(here, LANES - 1, 1))
            part_z_ = (flux_z - pltpu.roll(flux_z, 1, 1))[:, :bz]
            out = s_ref[c, a] * mid + (flux_high - flux_low) + (flux_y - flux_yd) + part_z_
            q[c, a] = out
            if with_dot:
                acc = acc + mid * out
            return above, flux_high, acc

        start = (first, flux_x(kx0[c], below, first), jnp.zeros((by, bz), jnp.float32))
        return lax.fori_loop(0, bx, body, start)[2]

    def kx_copy(c):
        return remote(kx_ref.at[c, bx - 1], kx0.at[c], init_ssem.at[1, c, 0], init_rsem.at[1, c, 0], x_up)

    def ky_copy(c):
        return remote(yi_send.at[1, c, 0], yi_recv.at[1, c, 0], init_ssem.at[1, c, 1], init_rsem.at[1, c, 1], y_up)

    def kz_copy(c):
        return remote(zi_send.at[1, c], zi_recv.at[1, c, 0], init_ssem.at[1, c, 2], init_rsem.at[1, c, 2], z_up)

    for c in range(SYS):
        kx_copy(c).start()

        def fill(a, carry, c=c):
            value = x0_ref[c, a]
            x_ref[c, a] = value
            p[c, a + 1, ROW0:ROW0 + by, :bz] = value
            cond = ky_ref[c, a]
            kyd[c, a, 1:by, :] = cond[:by - 1, :]
            yi_send[1, c, 0, a, :, :bz] = cond[by - 1:by, :]
            kze[c, a, :, :bz] = kz_ref[c, a]
            return carry
        lax.fori_loop(0, bx, fill, 0)
        ky_copy(c).start()
        zi_send[1, c] = z_extract(lambda a, c=c: kze[c, a])
        kz_copy(c).start()
        halo_start(c, *x_halo)

    for c in range(SYS):
        rho_ref[c] = jnp.ones((1, LANES), jnp.float32)
        beta_ref[c] = jnp.zeros((1, LANES), jnp.float32)
        hist_ref[c] = jnp.zeros((1, LANES), jnp.float32)
        kx_copy(c).wait()
        ky_copy(c).wait()
        kz_copy(c).wait()

        def low_row(a, carry, c=c):
            kyd[c, a, 0:1, :] = yi_recv[1, c, 0, a, :, :bz]
            return carry
        lax.fori_loop(0, bx, low_row, 0, unroll=8)

        def store_low(a, lanes, c=c):
            kze[c, a, :, bz:] = lanes
        z_insert(zi_send[1, c], zi_recv[1, c, 0], zi_recv[1, c, 0], store_low)

    for c in range(SYS):
        halo_finish(c, *x_halo)
        apply(c, None, False)

        def first_residual(a, acc, c=c):
            res = b_ref[c, a] - q[c, a]
            r[c, a + 1, ROW0:ROW0 + by, :bz] = res
            return acc + res * res
        dot_start(c, RR0, lax.fori_loop(0, bx, first_residual, jnp.zeros((by, bz), jnp.float32)))
        halo_start(c, *r_halo)

    def record(c, k, rho):
        hist_ref[c] = jnp.where(lane_row == k, rho, hist_ref[c])

    def cg_step(k, carry):
        for c in range(SYS):
            halo_finish(c, *r_halo)

            @pl.when(k > 0)
            def _(c=c):
                rho = dot_wait(c, RR)
                beta_ref[c] = rho / rho_ref[c]
                rho_ref[c] = rho
                record(c, k, rho)
            dot_start(c, PQ, apply(c, beta_ref[c], True))

        alphas = []
        for c in range(SYS):
            @pl.when(k == 0)
            def _(c=c):
                rho = dot_wait(c, RR0)
                rho_ref[c] = rho
                record(c, 0, rho)
            alpha = rho_ref[c] / dot_wait(c, PQ)
            alphas.append(alpha)

            def residual(a, acc, c=c, alpha=alpha):
                res = r[c, a + 1, ROW0:ROW0 + by, :bz] - alpha[:, :bz] * q[c, a]
                r[c, a + 1, ROW0:ROW0 + by, :bz] = res
                return acc + res * res
            dot_start(c, RR, lax.fori_loop(0, bx, residual, jnp.zeros((by, bz), jnp.float32), unroll=2))
            halo_start(c, *r_halo)

        for c in range(SYS):
            def update(a, inner, c=c):
                x_ref[c, a] = x_ref[c, a] + alphas[c][:, :bz] * p[c, a + 1, ROW0:ROW0 + by, :bz]
                return inner
            lax.fori_loop(0, bx, update, 0, unroll=2)
        return carry

    lax.fori_loop(0, ITERS, cg_step, 0)

    for c in range(SYS):
        for copy in halo_copies(c, *r_halo):
            copy.wait()
        record(c, ITERS, dot_wait(c, RR))
        hist_out[c:c + 1, :] = jnp.sqrt(hist_ref[c] / cell_count)[:, :ITERS + 1]


def solution(mesh):
    axis_sizes = tuple(mesh.shape[axis_name] for axis_name in ('px', 'py', 'pz'))
    n_dev = axis_sizes[0] * axis_sizes[1] * axis_sizes[2]
    field_spec = P(None, 'px', 'py', 'pz')

    def local_solve(shift_diag, rhs_field, x_start, cond_x, cond_y, cond_z):
        block = x_start.shape[1:]
        bx, by, bz = block
        cell_count = bx * by * bz * n_dev
        f32 = jnp.float32
        vmem = pl.BlockSpec(memory_space=pltpu.VMEM)
        padded = (SYS, bx + 2, by + 2 * ROW0, LANES)
        scratch = [
            pltpu.VMEM(padded, f32), pltpu.VMEM(padded, f32),
            pltpu.VMEM((SYS,) + block, f32), pltpu.VMEM((SYS,) + block, f32),
            pltpu.VMEM((SYS, bx, by, LANES), f32), pltpu.VMEM((SYS, by, bz), f32),
            pltpu.VMEM((SYS, 3, 1, LANES), f32), pltpu.VMEM((SYS, 3, n_dev, 1, LANES), f32),
            pltpu.VMEM((SYS, 1, LANES), f32), pltpu.VMEM((SYS, 1, LANES), f32), pltpu.VMEM((SYS, 1, LANES), f32),
            pltpu.VMEM((SYS, 2, bx, 1, LANES), f32), pltpu.VMEM((SYS, 2, bx, 1, LANES), f32),
            pltpu.VMEM((SYS, by, LANES), f32), pltpu.VMEM((SYS, 2, by, LANES), f32),
            pltpu.VMEM((2, SYS, 2, bx, 1, LANES), f32), pltpu.VMEM((2, SYS, 2, bx, 1, LANES), f32),
            pltpu.VMEM((2, SYS, by, LANES), f32), pltpu.VMEM((2, SYS, 2, by, LANES), f32),
            pltpu.SemaphoreType.DMA((SYS, 3)), pltpu.SemaphoreType.DMA((SYS, 3)),
            pltpu.SemaphoreType.DMA((SYS, 6)), pltpu.SemaphoreType.DMA((SYS, 6)),
            pltpu.SemaphoreType.DMA((2, SYS, 6)), pltpu.SemaphoreType.DMA((2, SYS, 6)),
        ]
        return pl.pallas_call(
            functools.partial(cg_kernel, axis_sizes, block, float(cell_count)),
            out_shape=(jax.ShapeDtypeStruct(x_start.shape, f32), jax.ShapeDtypeStruct((SYS, ITERS + 1), f32)),
            in_specs=[vmem] * 6,
            out_specs=(vmem, vmem),
            scratch_shapes=scratch,
            compiler_params=pltpu.CompilerParams(has_side_effects=True, vmem_limit_bytes=62 * 1024 * 1024),
        )(shift_diag, rhs_field, x_start, cond_x, cond_y, cond_z)

    return jax.shard_map(local_solve, mesh=mesh, in_specs=(field_spec,) * 6, out_specs=(field_spec, P(None, None)), check_vma=False)
```

time: 3630 us -> 587 us (0.16)
  blocking collectives: 2670 us -> 0 us
  Pallas kernels: 0 us -> 583 us
  local copies, waits for them, and re-layouts: 348 us -> 3.79 us
  other arithmetic: 343 us -> 0 us
  starting transfers between devices: 251 us -> 0 us
    psum x41 -> x0, blocking collectives: 2670 us -> none  [global_dot(): return lax.psum(jnp.sum(left_vec * right_vec, axis=(1, 2, 3)), ALL_AXES)]
    pallas_call x0 -> x1, Pallas kernels: none -> 583 us  [local_solve(): pl.pallas_call(functools.partial(cg_kernel, axis_sizes, block, float(cell...]
    ppermute x129 -> x0, starting transfers between devices: 251 us -> none  [the longest x63 145 us: neighbour_planes(): from_below = lax.ppermute(last_plane, axis_name, up_pairs(axis_size))]
    slice x106 -> x0, local copies, waits for them, and re-layouts: 171 us -> none  [the longest x83 115 us: neighbour_planes(): first_plane = lax.slice_in_dim(field, 0, 1, axis=axis_dim)]
    reduce_sum x41 -> x0, other arithmetic: 170 us -> none  [global_dot(): return lax.psum(jnp.sum(left_vec * right_vec, axis=(1, 2, 3)), ALL_AXES)]
    mul x61 -> x0, other arithmetic: 117 us -> none  [apply_local(): cond_ext[axis_pos]]
    ppermute x43 -> x0, local copies, waits for them, and re-layouts: 98.9 us -> none  [the longest x21 48.6 us: neighbour_planes(): from_below = lax.ppermute(last_plane, axis_name, up_pairs(axis_size))]
    while x141 -> x0, local copies, waits for them, and re-layouts: 46.9 us -> none
  transfers between devices with their start and end apart: 129 -> 0, of which waited for: 0 -> 0; matrix products, arithmetic and copies ran while one was open for 8% -> 0% of each run, Pallas kernels for 0% -> 0%
where the time goes in v1:
time: 587 us
  Pallas kernels  583 us (99%)
    pallas_call x1, Pallas kernels, local_solve(): pl.pallas_call(functools.partial(cg_kernel, axis_sizes, block, float(cell...  583 us

profile of v1, /device:TPU:1, one launch (start us, length us, event | category | flops | bytes accessed | tf_op | source)
XLA Modules:
  0.0 587.1 jit_solution(6745849635632293139)
XLA Ops:
  0.6 582.6 %shard_map.77 = (f32[2,48,48,96]{3,2,1,0:T(8,128)}, f32[2,21]{1,0:T(2,128)}) custom-call(f32[2,48,48,96]{3,2,1,0:T(8,128)} %s_ref.1, f32[2,48,48,96]{3,2,1,0:T(8,128)} %b_ref.1, f32[2,48,48,96]{3,2,1,0:T(8,128)} %x0_ref.1, f32[2,48,48,96]{3,2,1,0:T(8,128)} %kx_ref.1, f32[2,48,48,96]{3,2,1,0:T(8,128)} %ky_ref.1, f32[2,48,48,96]{3,2,1,0:T(8,128)} %kz_ref.1), custom_call_target="tpu_custom_call" | custom-call | tf_op jit(solution)/shard_map/pallas_call | solution.py:311
  583.3 0.0 copy-start
  583.3 3.2 copy.10
  586.5 0.0 copy-done
  586.5 0.6 copy.11
Async XLA Ops:
  583.3 3.2 copy-start

commit v2 on v1

--- a/solution.py
+++ b/solution.py
@@ -13,6 +13,7 @@
 ROW0 = 8
 LANES = 128
 MESH = pl.DeviceIdType.MESH
+AHEAD = 8
 PQ, RR, RR0 = 0, 1, 2
 
 
@@ -25,13 +26,14 @@
 
 
 def cg_kernel(axis_sizes, block, cell_count,
-              s_ref, b_ref, x0_ref, kx_ref, ky_ref, kz_ref,
+              s_hbm, b_hbm, x0_hbm, kx_hbm, ky_hbm, kz_hbm,
               x_ref, hist_out,
-              r, p, q, kyd, kze, kx0,
+              s_ref, b_ref, kx_ref, ky_ref, kz_ref,
+              r, p, q, kyd, kze, kzd, kx0,
               dot_send, dot_recv, rho_ref, beta_ref, hist_ref,
               y_send, y_recv, z_send, z_recv,
               yi_send, yi_recv, zi_send, zi_recv,
-              dot_ssem, dot_rsem, halo_ssem, halo_rsem, init_ssem, init_rsem):
+              dot_ssem, dot_rsem, halo_ssem, halo_rsem, init_ssem, init_rsem, load_sem):
     nx, ny, nz = axis_sizes
     bx, by, bz = block
     n_dev = nx * ny * nz
@@ -156,28 +158,52 @@
             p[c, j] = new
             return new[ROW0:ROW0 + by, :]
 
-        def flux_x(conduct, low, high):
-            return conduct * (low[:, :bz] - high[:, :bz])
-
-        below, first = direction(0), direction(1)
-
-        def body(a, carry):
-            here, flux_low, acc = carry
-            above = direction(a + 2)
-            mid = here[:, :bz]
-            flux_high = flux_x(kx_ref[c, a], here, above)
+        def z_part(a):
+            here = direction(a + 1)
+            up = (here - pltpu.roll(here, LANES - 1, 1))[:, :bz]
+            down = (pltpu.roll(here, 1, 1) - here)[:, :bz]
+            q[c, a] = s_ref[c, a] * here[:, :bz] + (kz_ref[c, a] * up - kzd[c, a] * down)
+
+        def xy_part(a, carry):
+            mid, flux_low, acc = carry
+            above = p[c, a + 2, ROW0:ROW0 + by, :bz]
+            flux_high = kx_ref[c, a] * (mid - above)
             flux_y = ky_ref[c, a] * (mid - p[c, a + 1, ROW0 + 1:ROW0 + by + 1, :bz])
             flux_yd = kyd[c, a] * (p[c, a + 1, ROW0 - 1:ROW0 + by - 1, :bz] - mid)
-            flux_z = kze[c, a] * (here - pltpu.roll(here, LANES - 1, 1))
-            part_z_ = (flux_z - pltpu.roll(flux_z, 1, 1))[:, :bz]
-            out = s_ref[c, a] * mid + (flux_high - flux_low) + (flux_y - flux_yd) + part_z_
+            out = q[c, a] + (flux_high - flux_low) + (flux_y - flux_yd)
             q[c, a] = out
             if with_dot:
                 acc = acc + mid * out
             return above, flux_high, acc
 
-        start = (first, flux_x(kx0[c], below, first), jnp.zeros((by, bz), jnp.float32))
-        return lax.fori_loop(0, bx, body, start)[2]
+        def both(a, carry):
+            z_part(a + AHEAD)
+            return xy_part(a, carry)
+
+        direction(0)
+        direction(bx + 1)
+        for a in range(AHEAD):
+            z_part(a)
+        first = p[c, 1, ROW0:ROW0 + by, :bz]
+        carry = (first, kx0[c] * (p[c, 0, ROW0:ROW0 + by, :bz] - first), jnp.zeros((by, bz), jnp.float32))
+        carry = lax.fori_loop(0, bx - AHEAD, both, carry, unroll=8)
+        for a in range(bx - AHEAD, bx):
+            carry = xy_part(a, carry)
+        return carry[2]
+
+    def load(c, i):
+        pairs = ((x0_hbm, x_ref), (kx_hbm, kx_ref), (ky_hbm, ky_ref), (kz_hbm, kz_ref), (s_hbm, s_ref), (b_hbm, b_ref))
+        src, dst = pairs[i]
+        return pltpu.make_async_copy(src.at[c], dst.at[c], load_sem.at[c, i])
+
+    for i in range(6):
+        for c in range(SYS):
+            load(c, i).start()
+
+    barrier = pltpu.get_barrier_semaphore()
+    for flip, step_x, step_y, step_z in targets:
+        pl.semaphore_signal(barrier, inc=1, device_id=device(part_x[flip][step_x], part_y[step_y], part_z[step_z]), device_id_type=MESH)
+    pl.semaphore_wait(barrier, n_dev - 1)
 
     def kx_copy(c):
         return remote(kx_ref.at[c, bx - 1], kx0.at[c], init_ssem.at[1, c, 0], init_rsem.at[1, c, 0], x_up)
@@ -189,12 +215,21 @@
         return remote(zi_send.at[1, c], zi_recv.at[1, c, 0], init_ssem.at[1, c, 2], init_rsem.at[1, c, 2], z_up)
 
     for c in range(SYS):
+        load(c, 0).wait()
+
+        def fill_p(a, carry, c=c):
+            p[c, a + 1, ROW0:ROW0 + by, :bz] = x_ref[c, a]
+            return carry
+        lax.fori_loop(0, bx, fill_p, 0, unroll=2)
+        halo_start(c, *x_halo)
+
+    for c in range(SYS):
+        load(c, 1).wait()
         kx_copy(c).start()
+        load(c, 2).wait()
+        load(c, 3).wait()
 
         def fill(a, carry, c=c):
-            value = x0_ref[c, a]
-            x_ref[c, a] = value
-            p[c, a + 1, ROW0:ROW0 + by, :bz] = value
             cond = ky_ref[c, a]
             kyd[c, a, 1:by, :] = cond[:by - 1, :]
             yi_send[1, c, 0, a, :, :bz] = cond[by - 1:by, :]
@@ -204,7 +239,6 @@
         ky_copy(c).start()
         zi_send[1, c] = z_extract(lambda a, c=c: kze[c, a])
         kz_copy(c).start()
-        halo_start(c, *x_halo)
 
     for c in range(SYS):
         rho_ref[c] = jnp.ones((1, LANES), jnp.float32)
@@ -223,9 +257,16 @@
             kze[c, a, :, bz:] = lanes
         z_insert(zi_send[1, c], zi_recv[1, c, 0], zi_recv[1, c, 0], store_low)
 
+        def shift_z(a, carry, c=c):
+            kzd[c, a] = pltpu.roll(kze[c, a], 1, 1)[:, :bz]
+            return carry
+        lax.fori_loop(0, bx, shift_z, 0, unroll=8)
+
     for c in range(SYS):
         halo_finish(c, *x_halo)
+        load(c, 4).wait()
         apply(c, None, False)
+        load(c, 5).wait()
 
         def first_residual(a, acc, c=c):
             res = b_ref[c, a] - q[c, a]
@@ -295,9 +336,11 @@
         vmem = pl.BlockSpec(memory_space=pltpu.VMEM)
         padded = (SYS, bx + 2, by + 2 * ROW0, LANES)
         scratch = [
+            *[pltpu.VMEM((SYS,) + block, f32)] * 5,
             pltpu.VMEM(padded, f32), pltpu.VMEM(padded, f32),
             pltpu.VMEM((SYS,) + block, f32), pltpu.VMEM((SYS,) + block, f32),
-            pltpu.VMEM((SYS, bx, by, LANES), f32), pltpu.VMEM((SYS, by, bz), f32),
+            pltpu.VMEM((SYS, bx, by, LANES), f32), pltpu.VMEM((SYS,) + block, f32),
+            pltpu.VMEM((SYS, by, bz), f32),
             pltpu.VMEM((SYS, 3, 1, LANES), f32), pltpu.VMEM((SYS, 3, n_dev, 1, LANES), f32),
             pltpu.VMEM((SYS, 1, LANES), f32), pltpu.VMEM((SYS, 1, LANES), f32), pltpu.VMEM((SYS, 1, LANES), f32),
             pltpu.VMEM((SYS, 2, bx, 1, LANES), f32), pltpu.VMEM((SYS, 2, bx, 1, LANES), f32),
@@ -307,14 +350,15 @@
             pltpu.SemaphoreType.DMA((SYS, 3)), pltpu.SemaphoreType.DMA((SYS, 3)),
             pltpu.SemaphoreType.DMA((SYS, 6)), pltpu.SemaphoreType.DMA((SYS, 6)),
             pltpu.SemaphoreType.DMA((2, SYS, 6)), pltpu.SemaphoreType.DMA((2, SYS, 6)),
+            pltpu.SemaphoreType.DMA((SYS, 6)),
         ]
         return pl.pallas_call(
             functools.partial(cg_kernel, axis_sizes, block, float(cell_count)),
             out_shape=(jax.ShapeDtypeStruct(x_start.shape, f32), jax.ShapeDtypeStruct((SYS, ITERS + 1), f32)),
-            in_specs=[vmem] * 6,
+            in_specs=[pl.BlockSpec(memory_space=pl.ANY)] * 6,
             out_specs=(vmem, vmem),
             scratch_shapes=scratch,
-            compiler_params=pltpu.CompilerParams(has_side_effects=True, vmem_limit_bytes=62 * 1024 * 1024),
+            compiler_params=pltpu.CompilerParams(has_side_effects=True, collective_id=0, vmem_limit_bytes=62 * 1024 * 1024),
         )(shift_diag, rhs_field, x_start, cond_x, cond_y, cond_z)
 
     return jax.shard_map(local_solve, mesh=mesh, in_specs=(field_spec,) * 6, out_specs=(field_spec, P(None, None)), check_vma=False)

time: 587 us -> 331 us (0.56)
  Pallas kernels: 583 us -> 326 us
    pallas_call x1, Pallas kernels: 583 us -> 326 us  [local_solve(): pl.pallas_call(functools.partial(cg_kernel, axis_sizes, block, float(cell...]
where the time goes in v2:
time: 331 us
  Pallas kernels  326 us (98%)
  local copies, waits for them, and re-layouts  3.79 us (1%)
    pallas_call x1, Pallas kernels, local_solve(): pl.pallas_call(functools.partial(cg_kernel, axis_sizes, block, float(cell...  326 us

profile of v2, /device:TPU:1, one launch (start us, length us, event | category | flops | bytes accessed | tf_op | source)
XLA Modules:
  0.0 330.9 jit_solution(11812499163384247541)
XLA Ops:
  0.6 326.4 %shard_map.77 = (f32[2,48,48,96]{3,2,1,0:T(8,128)}, f32[2,21]{1,0:T(2,128)}) custom-call(f32[2,48,48,96]{3,2,1,0:T(8,128)} %s_hbm.1, f32[2,48,48,96]{3,2,1,0:T(8,128)} %b_hbm.1, f32[2,48,48,96]{3,2,1,0:T(8,128)} %x0_hbm.1, f32[2,48,48,96]{3,2,1,0:T(8,128)} %kx_hbm.1, f32[2,48,48,96]{3,2,1,0:T(8,128)} %ky_hbm.1, f32[2,48,48,96]{3,2,1,0:T(8,128)} %kz_hbm.1), custom_call_target="tpu_custom_call" | custom-call | tf_op jit(solution)/shard_map/pallas_call | solution.py:355
  327.1 0.0 copy-start
  327.1 3.2 copy.10
  330.3 0.0 copy-done
  330.3 0.6 copy.11
Async XLA Ops:
  327.1 3.2 copy-start

commit v3 on v2

--- a/solution.py
+++ b/solution.py
@@ -13,7 +13,7 @@
 ROW0 = 8
 LANES = 128
 MESH = pl.DeviceIdType.MESH
-AHEAD = 8
+UNROLL = 12
 PQ, RR, RR0 = 0, 1, 2
 
 
@@ -73,7 +73,10 @@
         others = dot_recv.at[c, slot, pl.ds(0, n_dev - 1)]
         pltpu.make_async_copy(others, others, dot_rsem.at[c, slot]).wait()
         pltpu.make_async_copy(others, others, dot_ssem.at[c, slot]).wait()
-        return jnp.sum(dot_recv[c, slot], axis=0)
+        terms = [dot_recv[c, slot, i] for i in range(n_dev)]
+        while len(terms) > 1:
+            terms = [low + high for low, high in zip(terms[0::2], terms[1::2])]
+        return terms[0]
 
     def z_shift(a):
         return a + 33 + jnp.where(a >= half, 64 - half, 0)
@@ -109,21 +112,22 @@
             remote(zs.at[c], zr.at[c, 1], ssem.at[c, 5], rsem.at[c, 5], z_up),
         ]
 
-    def halo_start(c, field, ys, yr, zs, zr, ssem, rsem):
-        copies = halo_copies(c, field, ys, yr, zs, zr, ssem, rsem)
-        copies[0].start()
-        copies[1].start()
+    def halo_start(c, field, ys, yr, zs, zr, ssem, rsem, send=True):
+        copies = halo_copies(c, field, ys, yr, zs, zr, ssem, rsem) if send else []
+
+        def start(which):
+            for copy in copies[which:which + 2]:
+                copy.start()
+        start(0)
 
         def pack(a, carry):
             ys[c, 0, a] = field[c, a + 1, ROW0:ROW0 + 1, :]
             ys[c, 1, a] = field[c, a + 1, ROW0 + by - 1:ROW0 + by, :]
             return carry
         lax.fori_loop(0, bx, pack, 0, unroll=8)
-        copies[2].start()
-        copies[3].start()
+        start(2)
         zs[c] = z_extract(lambda a: field[c, a + 1, ROW0:ROW0 + by, :])
-        copies[4].start()
-        copies[5].start()
+        start(4)
 
     def halo_finish(c, field, ys, yr, zs, zr, ssem, rsem):
         for copy in halo_copies(c, field, ys, yr, zs, zr, ssem, rsem):
@@ -158,38 +162,24 @@
             p[c, j] = new
             return new[ROW0:ROW0 + by, :]
 
-        def z_part(a):
-            here = direction(a + 1)
+        def body(a, carry):
+            here, flux_low, acc = carry
+            above = direction(a + 2)
+            mid = here[:, :bz]
             up = (here - pltpu.roll(here, LANES - 1, 1))[:, :bz]
             down = (pltpu.roll(here, 1, 1) - here)[:, :bz]
-            q[c, a] = s_ref[c, a] * here[:, :bz] + (kz_ref[c, a] * up - kzd[c, a] * down)
-
-        def xy_part(a, carry):
-            mid, flux_low, acc = carry
-            above = p[c, a + 2, ROW0:ROW0 + by, :bz]
-            flux_high = kx_ref[c, a] * (mid - above)
+            flux_high = kx_ref[c, a] * (mid - above[:, :bz])
             flux_y = ky_ref[c, a] * (mid - p[c, a + 1, ROW0 + 1:ROW0 + by + 1, :bz])
             flux_yd = kyd[c, a] * (p[c, a + 1, ROW0 - 1:ROW0 + by - 1, :bz] - mid)
-            out = q[c, a] + (flux_high - flux_low) + (flux_y - flux_yd)
+            out = s_ref[c, a] * mid + (flux_high - flux_low) + (flux_y - flux_yd) + (kz_ref[c, a] * up - kzd[c, a] * down)
             q[c, a] = out
             if with_dot:
                 acc = acc + mid * out
             return above, flux_high, acc
 
-        def both(a, carry):
-            z_part(a + AHEAD)
-            return xy_part(a, carry)
-
-        direction(0)
-        direction(bx + 1)
-        for a in range(AHEAD):
-            z_part(a)
-        first = p[c, 1, ROW0:ROW0 + by, :bz]
-        carry = (first, kx0[c] * (p[c, 0, ROW0:ROW0 + by, :bz] - first), jnp.zeros((by, bz), jnp.float32))
-        carry = lax.fori_loop(0, bx - AHEAD, both, carry, unroll=8)
-        for a in range(bx - AHEAD, bx):
-            carry = xy_part(a, carry)
-        return carry[2]
+        below, first = direction(0), direction(1)
+        carry = (first, kx0[c] * (below[:, :bz] - first[:, :bz]), jnp.zeros((by, bz), jnp.float32))
+        return lax.fori_loop(0, bx, body, carry, unroll=UNROLL)[2]
 
     def load(c, i):
         pairs = ((x0_hbm, x_ref), (kx_hbm, kx_ref), (ky_hbm, ky_ref), (kz_hbm, kz_ref), (s_hbm, s_ref), (b_hbm, b_ref))
@@ -203,8 +193,6 @@
     barrier = pltpu.get_barrier_semaphore()
     for flip, step_x, step_y, step_z in targets:
         pl.semaphore_signal(barrier, inc=1, device_id=device(part_x[flip][step_x], part_y[step_y], part_z[step_z]), device_id_type=MESH)
-    pl.semaphore_wait(barrier, n_dev - 1)
-
     def kx_copy(c):
         return remote(kx_ref.at[c, bx - 1], kx0.at[c], init_ssem.at[1, c, 0], init_rsem.at[1, c, 0], x_up)
 
@@ -221,11 +209,10 @@
             p[c, a + 1, ROW0:ROW0 + by, :bz] = x_ref[c, a]
             return carry
         lax.fori_loop(0, bx, fill_p, 0, unroll=2)
-        halo_start(c, *x_halo)
+        halo_start(c, *x_halo, send=False)
 
     for c in range(SYS):
         load(c, 1).wait()
-        kx_copy(c).start()
         load(c, 2).wait()
         load(c, 3).wait()
 
@@ -235,10 +222,16 @@
             yi_send[1, c, 0, a, :, :bz] = cond[by - 1:by, :]
             kze[c, a, :, :bz] = kz_ref[c, a]
             return carry
-        lax.fori_loop(0, bx, fill, 0)
+        lax.fori_loop(0, bx, fill, 0, unroll=4)
+        zi_send[1, c] = z_extract(lambda a, c=c: kze[c, a])
+
+    pl.semaphore_wait(barrier, n_dev - 1)
+    for c in range(SYS):
+        kx_copy(c).start()
         ky_copy(c).start()
-        zi_send[1, c] = z_extract(lambda a, c=c: kze[c, a])
         kz_copy(c).start()
+        for copy in halo_copies(c, *x_halo):
+            copy.start()
 
     for c in range(SYS):
         rho_ref[c] = jnp.ones((1, LANES), jnp.float32)
@@ -272,7 +265,7 @@
             res = b_ref[c, a] - q[c, a]
             r[c, a + 1, ROW0:ROW0 + by, :bz] = res
             return acc + res * res
-        dot_start(c, RR0, lax.fori_loop(0, bx, first_residual, jnp.zeros((by, bz), jnp.float32)))
+        dot_start(c, RR0, lax.fori_loop(0, bx, first_residual, jnp.zeros((by, bz), jnp.float32), unroll=6))
         halo_start(c, *r_halo)
 
     def record(c, k, rho):
@@ -304,7 +297,7 @@
                 res = r[c, a + 1, ROW0:ROW0 + by, :bz] - alpha[:, :bz] * q[c, a]
                 r[c, a + 1, ROW0:ROW0 + by, :bz] = res
                 return acc + res * res
-            dot_start(c, RR, lax.fori_loop(0, bx, residual, jnp.zeros((by, bz), jnp.float32), unroll=2))
+            dot_start(c, RR, lax.fori_loop(0, bx, residual, jnp.zeros((by, bz), jnp.float32), unroll=6))
             halo_start(c, *r_halo)
 
         for c in range(SYS):

time: 331 us -> 310 us (0.937)
  Pallas kernels: 326 us -> 306 us
    pallas_call x1, Pallas kernels: 326 us -> 306 us  [local_solve(): pl.pallas_call(functools.partial(cg_kernel, axis_sizes, block, float(cell...]
where the time goes in v3:
time: 310 us
  Pallas kernels  306 us (99%)
  local copies, waits for them, and re-layouts  3.79 us (1%)
    pallas_call x1, Pallas kernels, local_solve(): pl.pallas_call(functools.partial(cg_kernel, axis_sizes, block, float(cell...  306 us

profile of v3, /device:TPU:1, one launch (start us, length us, event | category | flops | bytes accessed | tf_op | source)
XLA Modules:
  0.0 310.1 jit_solution(3102562116251615705)
XLA Ops:
  0.6 305.7 %shard_map.77 = (f32[2,48,48,96]{3,2,1,0:T(8,128)}, f32[2,21]{1,0:T(2,128)}) custom-call(f32[2,48,48,96]{3,2,1,0:T(8,128)} %s_hbm.1, f32[2,48,48,96]{3,2,1,0:T(8,128)} %b_hbm.1, f32[2,48,48,96]{3,2,1,0:T(8,128)} %x0_hbm.1, f32[2,48,48,96]{3,2,1,0:T(8,128)} %kx_hbm.1, f32[2,48,48,96]{3,2,1,0:T(8,128)} %ky_hbm.1, f32[2,48,48,96]{3,2,1,0:T(8,128)} %kz_hbm.1), custom_call_target="tpu_custom_call" | custom-call | tf_op jit(solution)/shard_map/pallas_call | solution.py:348
  306.3 0.0 copy-start
  306.4 3.2 %copy.10 = f32[2,48,48,96]{3,2,1,0:T(8,128)} copy(f32[2,48,48,96]{3,2,1,0:T(8,128)} %get-tuple-element.4) | data formatting | bytes 3538944
  309.6 0.0 copy-done
  309.6 0.6 copy.11
Async XLA Ops:
  306.3 3.2 %copy-start = (f32[2,21]{1,0:T(2,128)S(1)}, f32[2,21]{1,0:T(2,128)}, u32[]{:S(2)}) copy-start(f32[2,21]{1,0:T(2,128)} %get-tuple-element.5) | copy-start | bytes 508
